TPU v7x, 32 devices: a whole 2x2x4 slice. The times are simulated.
32 devices in a mesh: section: 2 (over core), dp: 4 (over y, x), tensor: 4 (over z).
Axes of the slice: x: 2, y: 2, z: 4, core: 2. Of those that a mesh axis runs over, the one named last changes fastest.
Arguments:
- tokens_in: bfloat16 [512, 8192], P('dp', ('section', 'tensor')), may hold values from -70 to 70
- gain_attn: bfloat16 [8192], replicated, may hold values from 0.5 to 1.5
- w_query: bfloat16 [8192, 8192], P(None, ('section', 'tensor')), may hold values from -6 to 6
- w_keyval: bfloat16 [8192, 2048], P(None, ('section', 'tensor')), may hold values from -0.0625 to 0.0625
- w_out: bfloat16 [8192, 8192], P(('section', 'tensor')), may hold values from -0.0625 to 0.0625
- gain_mlp: bfloat16 [8192], replicated, may hold values from 0.5 to 1.5
- w_gate: bfloat16 [8192, 16384], P('dp', ('section', 'tensor')), may hold values from -0.0625 to 0.0625
- w_up: bfloat16 [8192, 16384], P('dp', ('section', 'tensor')), may hold values from -0.0625 to 0.0625
- w_down: bfloat16 [16384, 8192], P(('section', 'tensor'), 'dp'), may hold values from -0.046875 to 0.046875
Outputs:
- layer_out: bfloat16 [512, 8192], P(('section', 'tensor'), 'dp')
All inputs are finite; a program needn't handle non-finite values.
Results may differ from a plain program's by a relative error of at most 0.0068.
Values may be sent and summed in bfloat16 or wider, within the bound.
A program may use at most 128 MiB of HBM per device.

v0:
```python
import jax
import jax.numpy as jnp
from jax import lax
from jax.sharding import PartitionSpec as P

H = 64
KVH = 8
HD = 128


EPS = 1e-05
THETA = 10000.0


def rms_scale(row_data, gain_row):
    values = row_data.astype(jnp.float32)
    factor = lax.rsqrt(jnp.mean(values * values, axis=-1, keepdims=True) + EPS)
    return (values * factor * gain_row.astype(jnp.float32)).astype(jnp.bfloat16)


def rotary(values, positions):
    half_dim = values.shape[-1] // 2
    frequency = THETA ** (-jnp.arange(half_dim, dtype=jnp.float32) * 2.0 / values.shape[-1])
    angles = positions.astype(jnp.float32)[:, None] * frequency[None, :]
    cosine = jnp.cos(angles)[:, None, :]
    sine_part = jnp.sin(angles)[:, None, :]
    first_half = values[..., :half_dim]
    second = values[..., half_dim:]
    return jnp.concatenate(
        [first_half * cosine - second * sine_part, second * cosine + first_half * sine_part],
        axis=-1,
    )


def shards(tokens_in, gain_attn, w_query, w_keyval, w_out, gain_mlp, w_gate, w_up, w_down):
    group_count = lax.axis_size(("section", "tensor"))
    group_index = lax.axis_index(("section", "tensor"))
    data_index = lax.axis_index("dp")
    local_rows = tokens_in.shape[0]
    full_rows = lax.all_gather(tokens_in, ("section", "tensor"), axis=1, tiled=True)
    normed_attn = rms_scale(full_rows, gain_attn)
    heads_dev = w_query.shape[1] // HD
    group_size = H // KVH
    kv_dev = max(1, heads_dev // group_size)
    positions_local = data_index * local_rows + jnp.arange(local_rows, dtype=jnp.int32)
    query_proj = jnp.dot(normed_attn, w_query, preferred_element_type=jnp.float32)
    query_rot = rotary(query_proj.reshape(local_rows, heads_dev, HD), positions_local).astype(
        jnp.bfloat16
    )
    keyval_part = jnp.dot(normed_attn, w_keyval, preferred_element_type=jnp.float32).astype(
        jnp.bfloat16
    )
    keyval_rows = lax.all_gather(keyval_part, ("section", "tensor"), axis=1, tiled=True)
    first_kv = group_index * heads_dev // group_size
    key_cols = lax.dynamic_slice_in_dim(keyval_rows, first_kv * HD, kv_dev * HD, 1)
    value_cols = lax.dynamic_slice_in_dim(keyval_rows, KVH * HD + first_kv * HD, kv_dev * HD, 1)
    needed = jnp.concatenate([key_cols, value_cols], axis=1)
    kv_all = lax.all_gather(needed, "dp", axis=0, tiled=True)
    total_rows = kv_all.shape[0]
    key_pos = jnp.arange(total_rows, dtype=jnp.int32)
    key_rot = rotary(
        kv_all[:, : kv_dev * HD].astype(jnp.float32).reshape(total_rows, kv_dev, HD), key_pos
    ).astype(jnp.bfloat16)
    value_all = kv_all[:, kv_dev * HD :].reshape(total_rows, kv_dev, HD)
    query_grp = query_rot.reshape(local_rows, kv_dev, heads_dev // kv_dev, HD)
    scores = jnp.einsum(
        "rkgd,skd->kgrs", query_grp, key_rot, preferred_element_type=jnp.float32
    ) * HD ** (-0.5)
    allowed = key_pos[None, :] <= positions_local[:, None]
    scores = jnp.where(allowed[None, None, :, :], scores, -1e30)
    row_peak = jnp.max(scores, axis=-1, keepdims=True)
    expo_rows = jnp.exp(scores - row_peak)
    prob_rows = (expo_rows / jnp.sum(expo_rows, axis=-1, keepdims=True)).astype(jnp.bfloat16)
    attended = jnp.einsum(
        "kgrs,skd->rkgd", prob_rows, value_all, preferred_element_type=jnp.float32
    )
    attended = attended.astype(jnp.bfloat16).reshape(local_rows, heads_dev * HD)
    head_terms = jnp.dot(attended, w_out, preferred_element_type=jnp.float32)
    summed = lax.psum(head_terms, ("section", "tensor"))
    mid_full = (full_rows.astype(jnp.float32) + summed).astype(jnp.bfloat16)
    normed_mlp = rms_scale(mid_full, gain_mlp)
    mid_cols, norm_cols = (
        lax.all_to_all(mid_full, "dp", split_axis=1, concat_axis=0, tiled=True),
        lax.all_to_all(normed_mlp, "dp", split_axis=1, concat_axis=0, tiled=True),
    )
    hidden_width = w_gate.shape[1]
    row_block = norm_cols
    gate_block = jnp.dot(row_block, w_gate, preferred_element_type=jnp.float32)
    up_block = jnp.dot(row_block, w_up, preferred_element_type=jnp.float32)
    gate_both = lax.psum_scatter(
        jnp.concatenate([gate_block, up_block], axis=1), "dp", scatter_dimension=0, tiled=True
    )
    hidden_part = (jax.nn.silu(gate_both[:, :hidden_width]) * gate_both[:, hidden_width:]).astype(
        jnp.bfloat16
    )
    hidden_all = lax.all_gather(hidden_part, "dp", axis=0, tiled=True)
    out_rows = hidden_all.shape[0] // group_count
    row_block = hidden_all
    down_part = lax.psum_scatter(
        jnp.dot(row_block, w_down, preferred_element_type=jnp.float32),
        ("section", "tensor"),
        scatter_dimension=0,
        tiled=True,
    )
    resid_rows = lax.dynamic_slice_in_dim(mid_cols, group_index * out_rows, out_rows, 0)
    return (resid_rows.astype(jnp.float32) + down_part).astype(jnp.bfloat16)


def solution(mesh):
    placed = (
        P("dp", ("section", "tensor")),
        P(),
        P(None, ("section", "tensor")),
        P(None, ("section", "tensor")),
        P(("section", "tensor"), None),
        P(),
        P("dp", ("section", "tensor")),
        P("dp", ("section", "tensor")),
        P(("section", "tensor"), "dp"),
    )
    return jax.shard_map(
        shards,
        mesh=mesh,
        in_specs=placed,
        out_specs=P(("section", "tensor"), "dp"),
        check_vma=False,
    )
```

profile of v0, /device:TPU:25, one launch (start us, length us, event | category | flops | bytes accessed | tf_op | source)
XLA Modules:
  0.0 469.5 jit_solution(17559355887173237044)
XLA Ops:
  8.5 29.5 %all-gather.3.cloned.1.call-done = bf16[128,8192]{1,0:T(8,128)(2,1)} async-done(((bf16[128,1024]{1,0:T(8,128)(2,1)}), bf16[128,8192]{1,0:T(8,128)(2,1)}) %all-gather.3.cloned.1.call-update) | async-done | bytes 2097168 | tf_op jit(solution)/shard_map/all_gather | solution.py:40
  38.0 2.1 fusion.3
  40.1 3.7 convolution_convert_fusion.1
  43.8 26.3 %all_gather.13 = bf16[128,2048]{1,0:T(8,128)(2,1)S(1)} all-gather(bf16[128,256]{1,0:T(8,128)(2,1)S(1)} %convolution_convert_fusion.1), channel_id=1, replica_groups=mesh['section'=2,'dp'=4,'tensor'=4] {'section','tensor'}, dimensions={1}, use_global_device_ids=true | all-gather | bytes 589824 | tf_op jit(solution)/shard_map/all_gather | solution.py:53
  70.2 7.2 %all_gather.14 = bf16[512,256]{1,0:T(8,128)(2,1)S(1)} all-gather(bf16[128,256]{1,0:T(8,128)(2,1)S(1)} %pad_maximum_fusion.1), channel_id=1, replica_groups=mesh['section'=2,'dp'=4,'tensor'=4] {'dp'}, dimensions={0}, use_global_device_ids=true | all-gather | bytes 327680 | tf_op jit(solution)/shard_map/all_gather | solution.py:58
  77.4 8.4 %convolution_bitcast_fusion = f32[16,8,8,128]{3,1,2,0:T(8,128)S(1)} fusion(bf16[8192,1024]{1,0:T(8,128)(2,1)} %param.11, bf16[128,8192]{1,0:T(8,128)(2,1)S(1)} %copy-done, f32[8192]{0:T(1024)S(1)} %convert_element_type.75, f32[128]{0:T(128)S(1)} %add_rsqrt_fusion.1), kind=kOutput, calls=%fused_computation.19 | convolution fusion | flops 2151677952 | bytes 19431936 | tf_op jit(solution)/shard_map/dot_general | solution.py:46
  86.2 1.2 fusion.27
  89.1 0.7 slice-done.3
  89.8 4.8 %fusion.33 = f32[128,8192]{1,0:T(8,128)} fusion(bf16[128,1024]{0,1:T(8,128)(2,1)S(1)} %bitcast.66, bf16[1024,8192]{1,0:T(8,128)(2,1)S(1)} %bitcast.58), kind=kOutput, calls=%fused_computation.64 | convolution fusion | flops 2147483648 | bytes 21233664 | tf_op jit(solution)/shard_map/dot_general | solution.py:78
  95.4 96.7 %all-reduce.2.cloned.1.call-done = f32[128,8192]{1,0:T(8,128)} async-done(((f32[128,8192]{1,0:T(8,128)}), f32[128,8192]{1,0:T(8,128)}) %all-reduce.2.cloned.1.call-update) | async-done | bytes 4194320 | tf_op jit(solution)/shard_map/psum | solution.py:79
  192.1 3.7 fusion
  196.7 27.5 %all_to_all.38 = bf16[128,4,2048]{2,0,1:T(8,128)(2,1)S(1)} all-to-all(bf16[128,4,2048]{2,0,1:T(8,128)(2,1)S(1)} %bitcast.61), channel_id=1, replica_groups=mesh['section'=2,'dp'=4,'tensor'=4] {'dp'}, dimensions={1} | all-to-all | bytes 4194304 | tf_op jit(solution)/shard_map/all_to_all | solution.py:84
  224.2 4.6 fusion.35
  228.9 4.6 fusion.34
  233.5 3.8 pad_maximum_fusion
  237.3 87.3 %reduce-scatter.3.cloned.1.call-done = f32[128,4096]{1,0:T(8,128)} async-done(((f32[512,4096]{1,0:T(8,128)}), f32[128,4096]{1,0:T(8,128)}) %reduce-scatter.3.cloned.1.call-update) | async-done | bytes 2097168 | tf_op jit(solution)/shard_map/reduce_scatter | solution.py:90
  324.6 2.6 fusion.8
  327.3 35.3 %all-gather.5.cloned.1.call-done = bf16[512,2048]{1,0:T(8,128)(2,1)} async-done(((bf16[128,2048]{1,0:T(8,128)(2,1)}), bf16[512,2048]{1,0:T(8,128)(2,1)}) %all-gather.5.cloned.1.call-update) | async-done | bytes 2097168 | tf_op jit(solution)/shard_map/all_gather | solution.py:96
  362.5 10.5 %fusion.36 = f32[512,2048]{1,0:T(8,128)} fusion(bf16[512,2048]{1,0:T(8,128)(2,1)} %all-gather.5.cloned.1.call-done, bf16[2048,2048]{1,0:T(8,128)(2,1)} %param.17), kind=kOutput, calls=%fused_computation.67 | convolution fusion | flops 4294967296 | bytes 14680064 | tf_op jit(solution)/shard_map/dot_general | solution.py:100
  373.0 1.5 copy.42
  374.5 3.6 all-to-all-start
  378.1 24.4 %all-to-all-done = bf16[128,4,2048]{2,0,1:T(8,128)(2,1)S(1)} async-done(((bf16[128,4,2048]{2,0,1:T(8,128)(2,1)}), bf16[128,4,2048]{2,0,1:T(8,128)(2,1)S(1)}, u32[]{:S(2)}, u32[]{:S(2)}) %all-to-all-start) | async-done | bytes 2097184 | tf_op jit(solution)/shard_map/all_to_all | solution.py:83
  402.6 58.6 %reduce-scatter.5.cloned.1.call-done = f32[64,2048]{1,0:T(8,128)} async-done(((f32[512,2048]{1,0:T(8,128)}), f32[64,2048]{1,0:T(8,128)}) %reduce-scatter.5.cloned.1.call-update) | async-done | bytes 524304 | tf_op jit(solution)/shard_map/reduce_scatter | solution.py:99
  461.2 1.8 add_convert_fusion
  (53 shorter events, 5.6 us)
Async XLA Ops:
  6.5 31.4 %all-gather.3.cloned.1.call-start = ((), (), s32[]{:S(2)}) async-start(), calls=%async_computation.4 | async-start | bytes 2359296 | tf_op jit(solution)/shard_map/all_gather | solution.py:40
  7.3 184.8 %all-reduce.2.cloned.1.call-start = ((), (), s32[]{:S(2)}) async-start(), calls=%async_computation.5 | async-start | bytes 8388608 | tf_op jit(solution)/shard_map/psum | solution.py:79
  40.1 37.3 %copy-start = (bf16[128,8192]{1,0:T(8,128)(2,1)S(1)}, bf16[128,8192]{1,0:T(8,128)(2,1)}, u32[]{:S(2)}) copy-start(bf16[128,8192]{1,0:T(8,128)(2,1)} %all-gather.3.cloned.1.call-done) | copy-start | bytes 6291460
  77.4 11.6 %slice-start = ((s8[16777216]{0:T(1024)(128)(4,1)}), s8[4194304]{0:T(1024)(128)(4,1)S(1)}, s32[]{:S(2)}) async-start(s8[16777216]{0:T(1024)(128)(4,1)} %bitcast.57), calls=%async_computation.9 | async-start | bytes 8388608
  77.4 11.6 %slice-start.1 = ((s8[16777216]{0:T(1024)(128)(4,1)}), s8[4194304]{0:T(1024)(128)(4,1)S(1)}, s32[]{:S(2)}) async-start(s8[16777216]{0:T(1024)(128)(4,1)} %bitcast.57), calls=%async_computation.10 | async-start | bytes 8388608
  77.4 11.6 %slice-start.2 = ((s8[16777216]{0:T(1024)(128)(4,1)}), s8[4194304]{0:T(1024)(128)(4,1)S(1)}, s32[]{:S(2)}) async-start(s8[16777216]{0:T(1024)(128)(4,1)} %bitcast.57), calls=%async_computation.11 | async-start | bytes 8388608
  87.6 2.2 slice-start.3
  94.6 0.7 copy-start.1
  94.7 229.9 %reduce-scatter.3.cloned.1.call-start = ((), (), s32[]{:S(2)}) async-start(), calls=%async_computation.6 | async-start | bytes 10485760 | tf_op jit(solution)/shard_map/reduce_scatter | solution.py:90
  192.1 32.2 %slice-start.4 = ((s8[8388608]{0:T(1024)(128)(4,1)}), s8[4194304]{0:T(1024)(128)(4,1)S(1)}, s32[]{:S(2)}) async-start(s8[8388608]{0:T(1024)(128)(4,1)} %bitcast.67), calls=%async_computation.13 | async-start | bytes 8388608
  195.8 28.4 %slice-start.5 = ((s8[8388608]{0:T(1024)(128)(4,1)}), s8[4194304]{0:T(1024)(128)(4,1)S(1)}, s32[]{:S(2)}) async-start(s8[8388608]{0:T(1024)(128)(4,1)} %bitcast.67), calls=%async_computation.14 | async-start | bytes 8388608
  196.7 32.1 %slice-start.6 = ((s8[8388608]{0:T(1024)(128)(4,1)}), s8[4194304]{0:T(1024)(128)(4,1)S(1)}, s32[]{:S(2)}) async-start(s8[8388608]{0:T(1024)(128)(4,1)} %bitcast.69), calls=%async_computation.15 | async-start | bytes 8388608
  224.2 4.6 slice-start.7
  237.3 125.3 %all-gather.5.cloned.1.call-start = ((), (), s32[]{:S(2)}) async-start(), calls=%async_computation.7 | async-start | bytes 2621440 | tf_op jit(solution)/shard_map/all_gather | solution.py:96
  327.2 134.0 %reduce-scatter.5.cloned.1.call-start = ((), (), s32[]{:S(2)}) async-start(), calls=%async_computation.8 | async-start | bytes 4718592 | tf_op jit(solution)/shard_map/reduce_scatter | solution.py:99
  374.5 28.1 %all-to-all-start = ((bf16[128,4,2048]{2,0,1:T(8,128)(2,1)}), bf16[128,4,2048]{2,0,1:T(8,128)(2,1)S(1)}, u32[]{:S(2)}, u32[]{:S(2)}) async-start(bf16[128,4,2048]{2,0,1:T(8,128)(2,1)} %bitcast.59), calls=%async_computation | async-start | bytes 4194304 | tf_op jit(solution)/shard_map/all_to_all | solution.py:83
Sparse Core Ops, SparseCore 0:
  8.9 28.9 all-gather.2
  94.8 97.2 all-reduce.1
  237.4 87.1 reduce-scatter.2
  327.3 35.1 all-gather.4
  373.1 88.0 reduce-scatter.4
where the time goes:
time: 472 us; the launch traced here: 470 us
  waiting for transfers between devices  333 us (71%)
  blocking collectives  61 us (13%)
  matrix products  37.7 us (8%)
  other arithmetic  17.5 us (4%)
  between operations  13.5 us (3%)
    psum x1, waiting for transfers between devices, shards(): summed = lax.psum(head_terms, ('section', 'tensor'))  96.7 us
    reduce_scatter x1, waiting for transfers between devices, shards(): lax.psum_scatter(jnp.concatenate([gate_block, up_block], axis=1), 'dp', s...  87.3 us
    reduce_scatter x1, waiting for transfers between devices, shards(): lax.psum_scatter(jnp.dot(row_block, w_down, preferred_element_type=jnp.fl...  58.6 us
    all_gather x1, waiting for transfers between devices, shards(): hidden_all = lax.all_gather(hidden_part, 'dp', axis=0, tiled=True)  35.3 us
    all_gather x1, waiting for transfers between devices, shards(): lax.all_gather(tokens_in, ('section', 'tensor'), axis=1, tiled=True)  29.5 us
    all_to_all x1, blocking collectives, shards(): lax.all_to_all(normed_mlp, 'dp', split_axis=1, concat_axis=0, tiled=True)  27.5 us
    all_gather x1, blocking collectives, shards(): lax.all_gather(keyval_part, ('section', 'tensor'), axis=1, tiled=True)  26.3 us
    all_to_all x1, waiting for transfers between devices, shards(): lax.all_to_all(mid_full, 'dp', split_axis=1, concat_axis=0, tiled=True)  24.4 us
  transfers between devices with their start and end apart: 6, of which 6 were waited for; matrix products, arithmetic and copies ran while one was open for 1% of the time, Pallas kernels for 0%

commit v1 on v0

v1 whole, which is shorter than its diff:
```python
import functools

import jax
import jax.numpy as jnp
from jax import lax
from jax.experimental import pallas as pl
from jax.experimental.pallas import tpu as pltpu
from jax.sharding import PartitionSpec as P

H = 64
KVH = 8
HD = 128
EPS = 1e-05
THETA = 10000.0
CHUNKS = 4
MESH = pl.DeviceIdType.MESH
F32 = jnp.float32
BF16 = jnp.bfloat16
VMEM = pl.BlockSpec(memory_space=pltpu.VMEM)
ANY = pl.BlockSpec(memory_space=pl.ANY)


def rms_scale(row_data, gain_row):
    values = row_data.astype(jnp.float32)
    factor = lax.rsqrt(jnp.mean(values * values, axis=-1, keepdims=True) + EPS)
    return (values * factor * gain_row.astype(jnp.float32)).astype(jnp.bfloat16)


def rotary(values, positions):
    half_dim = values.shape[-1] // 2
    frequency = THETA ** (-jnp.arange(half_dim, dtype=jnp.float32) * 2.0 / values.shape[-1])
    angles = positions.astype(jnp.float32)[:, None] * frequency[None, :]
    cosine = jnp.cos(angles)[:, None, :]
    sine_part = jnp.sin(angles)[:, None, :]
    first_half = values[..., :half_dim]
    second = values[..., half_dim:]
    return jnp.concatenate(
        [first_half * cosine - second * sine_part, second * cosine + first_half * sine_part],
        axis=-1,
    )


def greet(peers):
    barrier = pltpu.get_barrier_semaphore()
    for peer in peers:
        pl.semaphore_signal(barrier, inc=1, device_id=peer, device_id_type=MESH)
    pl.semaphore_wait(barrier, len(peers))


def push(src, dst, sems, slot, device):
    return pltpu.make_async_remote_copy(
        src_ref=src,
        dst_ref=dst,
        send_sem=sems.at[0, slot],
        recv_sem=sems.at[1, slot],
        device_id=device,
        device_id_type=MESH,
    )


def others(axis):
    size = lax.axis_size(axis)
    me = lax.axis_index(axis)
    return [(step, lax.rem(me + step, size), lax.rem(me + size - step, size)) for step in range(1, size)]


def gather_group(out, at, sem_t, sem_s):
    section, tensor = lax.axis_index("section"), lax.axis_index("tensor")
    sections, tensors = others("section"), others("tensor")
    size_t = lax.axis_size("tensor")
    started = []

    def pass_on(block_t, slot):
        for step, to, _ in sections:
            block = out.at[at(section, block_t)]
            copy = push(block, block, sem_s, slot * len(sections) + step - 1, {"section": to})
            copy.start()
            started.append(copy)

    for step, to, _ in tensors:
        block = out.at[at(section, tensor)]
        copy = push(block, block, sem_t, step - 1, {"tensor": to})
        copy.start()
        started.append(copy)
    pass_on(tensor, 0)
    for step, to, source in tensors:
        block = out.at[at(section, source)]
        push(block, block, sem_t, step - 1, {"tensor": to}).wait_recv()
        pass_on(source, step)
    for slot in range(size_t):
        for step, to, source in sections:
            source_t = lax.rem(tensor + size_t - slot, size_t)
            block = out.at[at(source, source_t)]
            push(block, block, sem_s, slot * len(sections) + step - 1, {"section": to}).wait_recv()
    for copy in started:
        copy.wait_send()


def group_peers():
    return [{"tensor": to} for _, to, _ in others("tensor")] + [
        {"section": to} for _, to, _ in others("section")
    ]


def dma_sems(count):
    return pltpu.SemaphoreType.DMA((2, max(1, count)))


def ag_group_body(x_ref, out_ref, sem_t, sem_s, sem_local):
    section, tensor = lax.axis_index("section"), lax.axis_index("tensor")
    size_t = lax.axis_size("tensor")
    greet(group_peers())
    own = pltpu.make_async_copy(x_ref, out_ref.at[section * size_t + tensor], sem_local)
    own.start()
    own.wait()
    gather_group(out_ref, lambda s, t: s * size_t + t, sem_t, sem_s)


def ag_group(x, collective_id):
    size_s, size_t = lax.axis_size("section"), lax.axis_size("tensor")
    return pl.pallas_call(
        ag_group_body,
        out_shape=jax.ShapeDtypeStruct((size_s * size_t,) + x.shape, x.dtype),
        in_specs=[VMEM],
        out_specs=VMEM,
        scratch_shapes=[dma_sems(size_t - 1), dma_sems(size_t * (size_s - 1)), pltpu.SemaphoreType.DMA],
        compiler_params=pltpu.CompilerParams(collective_id=collective_id, has_side_effects=True),
    )(x)


def ag_dp_body(x_ref, out_ref, sem_d, sem_local):
    me = lax.axis_index("dp")
    greet([{"dp": to} for _, to, _ in others("dp")])
    own = pltpu.make_async_copy(x_ref, out_ref.at[me], sem_local)
    own.start()
    copies = []
    for step, to, _ in others("dp"):
        copy = push(x_ref, out_ref.at[me], sem_d, step - 1, {"dp": to})
        copy.start()
        copies.append(copy)
    own.wait()
    for step, to, source in others("dp"):
        push(x_ref, out_ref.at[source], sem_d, step - 1, {"dp": to}).wait_recv()
    for copy in copies:
        copy.wait_send()


def ag_dp(x, collective_id):
    size_d = lax.axis_size("dp")
    return pl.pallas_call(
        ag_dp_body,
        out_shape=jax.ShapeDtypeStruct((size_d,) + x.shape, x.dtype),
        in_specs=[VMEM],
        out_specs=VMEM,
        scratch_shapes=[dma_sems(size_d - 1), pltpu.SemaphoreType.DMA],
        compiler_params=pltpu.CompilerParams(collective_id=collective_id, has_side_effects=True),
    )(x)


def tile_of(width, most):
    return width if width <= most else most


def scatter_group(part, pair_rx, comb, z_rx, sem_p, sem_z):
    section, tensor = lax.axis_index("section"), lax.axis_index("tensor")
    size_t = lax.axis_size("tensor")
    block = z_rx.shape[1]

    def rows(s, t):
        return pl.ds(pl.multiple_of((s * size_t + t) * block, block), block)

    sections, tensors = others("section"), others("tensor")
    order = [(step, to) for step, to, _ in tensors] + [(0, tensor)]
    started = []
    for step, to in order:
        for hop, other, _ in sections:
            copy = push(
                part.at[rows(other, to)],
                pair_rx.at[hop - 1, step],
                sem_p,
                (hop - 1) * size_t + step,
                {"section": other},
            )
            copy.start()
            started.append(copy)

    def paired(step, to):
        total = part[rows(section, to), :].astype(F32)
        for hop, other, _ in sections:
            push(
                part.at[rows(other, to)],
                pair_rx.at[hop - 1, step],
                sem_p,
                (hop - 1) * size_t + step,
                {"section": other},
            ).wait_recv()
            total = total + pair_rx[hop - 1, step].astype(F32)
        return total

    for step, to, _ in tensors:
        comb[step - 1] = paired(step, to).astype(BF16)
        copy = push(comb.at[step - 1], z_rx.at[step - 1], sem_z, step - 1, {"tensor": to})
        copy.start()
        started.append(copy)
    total = paired(0, tensor)
    for step, to, _ in tensors:
        push(comb.at[step - 1], z_rx.at[step - 1], sem_z, step - 1, {"tensor": to}).wait_recv()
        total = total + z_rx[step - 1].astype(F32)
    for copy in started:
        copy.wait_send()
    return total


def back_body(
    att_ref, rows_ref, gain_ref, wo_hbm, wg_hbm, wu_hbm, wd_hbm, out_ref,
    wo, wg, wu, wd, att_all, part, pair_rx, comb, z_rx, resid, mid, stat_tx, stat_rx,
    nrm, gu, rx1, tx2, rx2, hid, acc, part2, pair_rx2, comb2, z_rx2,
    sem_w, sem_own, sem_att, sem_res, sem_p, sem_z, sem_stat, sem_t, sem_s,
    sem_1, sem_2, sem_h, sem_p2, sem_z2,
):
    section, tensor, me = lax.axis_index("section"), lax.axis_index("tensor"), lax.axis_index("dp")
    size_t, size_d = lax.axis_size("tensor"), lax.axis_size("dp")
    group_index = section * size_t + tensor
    local_rows, width = att_ref.shape
    block, cols = mid.shape
    total_rows = att_all.shape[0]
    features = rows_ref.shape[1]
    dps = others("dp")
    sends = []

    loads = [
        pltpu.make_async_copy(wo_hbm.at[:, pl.ds(pl.multiple_of(me * cols, cols), cols)], wo, sem_w.at[0]),
        pltpu.make_async_copy(wg_hbm, wg, sem_w.at[1]),
        pltpu.make_async_copy(wu_hbm, wu, sem_w.at[2]),
        pltpu.make_async_copy(wd_hbm, wd, sem_w.at[3]),
    ]
    for load in loads:
        load.start()

    greet(group_peers() + [{"dp": to} for _, to, _ in dps])

    def dp_rows(index):
        return pl.ds(pl.multiple_of(index * local_rows, local_rows), local_rows)

    for step, to, _ in dps:
        copy = push(att_ref, att_all.at[dp_rows(me)], sem_att, step - 1, {"dp": to})
        copy.start()
        sends.append(copy)

    per = local_rows // block
    holder = group_index // per
    held_rows = pl.ds(pl.multiple_of(lax.rem(group_index, per) * block, block), block)

    def resid_copy(step, to):
        src = rows_ref.at[held_rows, pl.ds(pl.multiple_of(to * cols, cols), cols)]
        return push(src, resid, sem_res, step - 1, {"dp": to})

    @pl.when(me == holder)
    def _():
        for step, to, _ in dps:
            resid_copy(step, to).start()
        resid[...] = rows_ref[held_rows, pl.ds(pl.multiple_of(me * cols, cols), cols)]

    att_all[dp_rows(me), :] = att_ref[...]
    loads[0].wait()
    tile = tile_of(cols, 512)

    def out_part(index):
        lines = att_all[dp_rows(index), :]

        @pl.loop(0, cols // tile)
        def _(j):
            at = pl.ds(pl.multiple_of(j * tile, tile), tile)
            part[dp_rows(index), at] = jnp.dot(lines, wo[:, at], preferred_element_type=F32).astype(BF16)

    out_part(me)
    for step, to, source in dps:
        push(att_ref, att_all.at[dp_rows(source)], sem_att, step - 1, {"dp": to}).wait_recv()
        out_part(source)

    summed = scatter_group(part, pair_rx, comb, z_rx, sem_p, sem_z)

    for step, to, source in dps:
        @pl.when(source == holder)
        def _():
            resid_copy(step, to).wait_recv()

    @pl.when(me == holder)
    def _():
        for step, to, _ in dps:
            resid_copy(step, to).wait_send()

    mid_rows = (resid[...].astype(F32) + summed).astype(BF16)
    mid[...] = mid_rows
    squares = mid_rows.astype(F32)
    stat = jnp.sum(squares * squares, axis=-1, keepdims=True)
    stat_tx[...] = jnp.broadcast_to(stat, stat_tx.shape)
    for step, to, _ in dps:
        copy = push(stat_tx, stat_rx.at[step - 1], sem_stat, step - 1, {"dp": to})
        copy.start()
        sends.append(copy)
    for step, to, _ in dps:
        push(stat_tx, stat_rx.at[step - 1], sem_stat, step - 1, {"dp": to}).wait_recv()
        stat = stat + stat_rx[step - 1][:, :1]
    factor = lax.rsqrt(stat * (1.0 / features) + EPS)

    def token_rows(s, t):
        return pl.ds(pl.multiple_of((s * size_t + t) * block, block), block)

    nrm[token_rows(section, tensor), :] = (
        mid[...].astype(F32) * factor * gain_ref[...].astype(F32)
    ).astype(BF16)
    gather_group(nrm, token_rows, sem_t, sem_s)

    loads[1].wait()
    loads[2].wait()
    share = gu.shape[2] // 2
    gtile = tile_of(share, 256)
    square = size_d == 4
    if square:
        x, y = lax.rem(me, 2), me // 2
        near = [y * 2 + (1 - x), (1 - y) * 2 + x]
        far = (1 - y) * 2 + (1 - x)
    for c in range(CHUNKS):
        @pl.loop(0, share // gtile)
        def _(j):
            src = pl.ds(pl.multiple_of(c * share + j * gtile, gtile), gtile)
            lo = pl.ds(pl.multiple_of(j * gtile, gtile), gtile)
            hi = pl.ds(pl.multiple_of(share + j * gtile, gtile), gtile)
            gu[c, :, lo] = jnp.dot(nrm[...], wg[:, src], preferred_element_type=F32).astype(BF16)
            gu[c, :, hi] = jnp.dot(nrm[...], wu[:, src], preferred_element_type=F32).astype(BF16)

        if square:
            first = near[c % 2]
            for slot, owner in ((1, far), (0, first)):
                copy = push(gu.at[c, dp_rows(owner)], rx1.at[c, slot], sem_1, 2 * c + slot, {"dp": first})
                copy.start()
                sends.append(copy)
        else:
            for step, to, _ in dps:
                slot = step - 1
                copy = push(gu.at[c, dp_rows(to)], rx1.at[c, slot], sem_1, (size_d - 1) * c + slot, {"dp": to})
                copy.start()
                sends.append(copy)

    if square:
        for c in range(CHUNKS):
            first, second = near[c % 2], near[1 - c % 2]
            push(gu.at[c, dp_rows(far)], rx1.at[c, 1], sem_1, 2 * c + 1, {"dp": first}).wait_recv()
            tx2[c] = (gu[c, dp_rows(second), :].astype(F32) + rx1[c, 1].astype(F32)).astype(BF16)
            copy = push(tx2.at[c], rx2.at[c], sem_2, c, {"dp": second})
            copy.start()
            sends.append(copy)

    hid_slots = size_d - 1
    for c in range(CHUNKS):
        both = gu[c, dp_rows(me), :].astype(F32)
        if square:
            first, second = near[c % 2], near[1 - c % 2]
            push(gu.at[c, dp_rows(first)], rx1.at[c, 0], sem_1, 2 * c, {"dp": first}).wait_recv()
            push(tx2.at[c], rx2.at[c], sem_2, c, {"dp": second}).wait_recv()
            both = both + rx1[c, 0].astype(F32) + rx2[c].astype(F32)
        else:
            for step, to, _ in dps:
                slot = step - 1
                push(
                    gu.at[c, dp_rows(to)], rx1.at[c, slot], sem_1, (size_d - 1) * c + slot, {"dp": to}
                ).wait_recv()
                both = both + rx1[c, slot].astype(F32)
        gate, up = both[:, :share], both[:, share:]
        hid[c, dp_rows(me), :] = (gate / (1.0 + jnp.exp(-gate)) * up).astype(BF16)
        mine = hid.at[c, dp_rows(me)]
        targets = list(enumerate(near)) if square else [(step - 1, to) for step, to, _ in dps]
        for slot, to in targets:
            copy = push(mine, mine, sem_h, hid_slots * c + slot, {"dp": to})
            copy.start()
            sends.append(copy)

    if square:
        for c in range(CHUNKS):
            one, two = c % 2, 1 - c % 2
            theirs = hid.at[c, dp_rows(near[one])]
            push(theirs, theirs, sem_h, hid_slots * c + one, {"dp": near[one]}).wait_recv()
            copy = push(theirs, theirs, sem_h, hid_slots * c + 2, {"dp": near[two]})
            copy.start()
            sends.append(copy)

    loads[3].wait()
    for c in range(CHUNKS):
        if square:
            two = 1 - c % 2
            arrivals = [(two, near[two]), (2, far)]
        else:
            arrivals = [(step - 1, source) for step, _, source in dps]
        for slot, source in arrivals:
            theirs = hid.at[c, dp_rows(source)]
            push(theirs, theirs, sem_h, hid_slots * c + slot, {"dp": source}).wait_recv()

        @pl.loop(0, cols // tile)
        def _(j):
            at = pl.ds(pl.multiple_of(j * tile, tile), tile)
            term = jnp.dot(hid[c], wd[c * share : (c + 1) * share, at], preferred_element_type=F32)
            if c > 0:
                term = acc[:, at] + term
            if c < CHUNKS - 1:
                acc[:, at] = term
            else:
                part2[:, at] = term.astype(BF16)

    total = scatter_group(part2, pair_rx2, comb2, z_rx2, sem_p2, sem_z2)
    out_ref[...] = (mid[...].astype(F32) + total).astype(BF16)
    for copy in sends:
        copy.wait_send()


def back(attended, full_rows, gain, w_out, w_gate, w_up, w_down, collective_id):
    size_s, size_t, size_d = lax.axis_size("section"), lax.axis_size("tensor"), lax.axis_size("dp")
    local_rows, width = attended.shape
    total_rows = local_rows * size_d
    block = total_rows // (size_s * size_t)
    cols, hidden = w_gate.shape
    share = hidden // CHUNKS
    slots = 2 if size_d == 4 else size_d - 1
    scatter = [
        pltpu.VMEM((total_rows, cols), BF16),
        pltpu.VMEM((size_s - 1, size_t, block, cols), BF16),
        pltpu.VMEM((size_t - 1, block, cols), BF16),
        pltpu.VMEM((size_t - 1, block, cols), BF16),
    ]
    return pl.pallas_call(
        back_body,
        out_shape=jax.ShapeDtypeStruct((block, cols), BF16),
        in_specs=[VMEM, VMEM, VMEM, ANY, ANY, ANY, ANY],
        out_specs=VMEM,
        scratch_shapes=[
            pltpu.VMEM((width, cols), BF16),
            pltpu.VMEM(w_gate.shape, BF16),
            pltpu.VMEM(w_up.shape, BF16),
            pltpu.VMEM(w_down.shape, BF16),
            pltpu.VMEM((total_rows, width), BF16),
            *scatter,
            pltpu.VMEM((block, cols), BF16),
            pltpu.VMEM((block, cols), BF16),
            pltpu.VMEM((block, 128), F32),
            pltpu.VMEM((size_d - 1, block, 128), F32),
            pltpu.VMEM((total_rows, cols), BF16),
            pltpu.VMEM((CHUNKS, total_rows, 2 * share), BF16),
            pltpu.VMEM((CHUNKS, slots, local_rows, 2 * share), BF16),
            pltpu.VMEM((CHUNKS, local_rows, 2 * share), BF16),
            pltpu.VMEM((CHUNKS, local_rows, 2 * share), BF16),
            pltpu.VMEM((CHUNKS, total_rows, share), BF16),
            pltpu.VMEM((total_rows, cols), F32),
            *scatter,
            pltpu.SemaphoreType.DMA((4,)),
            pltpu.SemaphoreType.DMA,
            dma_sems(size_d - 1),
            dma_sems(size_d - 1),
            dma_sems((size_s - 1) * size_t),
            dma_sems(size_t - 1),
            dma_sems(size_d - 1),
            dma_sems(size_t - 1),
            dma_sems(size_t * (size_s - 1)),
            dma_sems(CHUNKS * slots),
            dma_sems(CHUNKS),
            dma_sems(CHUNKS * (size_d - 1)),
            dma_sems((size_s - 1) * size_t),
            dma_sems(size_t - 1),
        ],
        compiler_params=pltpu.CompilerParams(
            collective_id=collective_id, has_side_effects=True, vmem_limit_bytes=66000000
        ),
    )(attended, full_rows, gain, w_out, w_gate, w_up, w_down)


def shards(tokens_in, gain_attn, w_query, w_keyval, w_out, gain_mlp, w_gate, w_up, w_down):
    group_index = lax.axis_index(("section", "tensor"))
    data_index = lax.axis_index("dp")
    local_rows = tokens_in.shape[0]
    gathered = ag_group(tokens_in, 1)
    full_rows = jnp.transpose(gathered, (1, 0, 2)).reshape(local_rows, -1)
    normed_attn = rms_scale(full_rows, gain_attn)
    heads_dev = w_query.shape[1] // HD
    group_size = H // KVH
    kv_dev = max(1, heads_dev // group_size)
    positions_local = data_index * local_rows + jnp.arange(local_rows, dtype=jnp.int32)
    keyval_part = jnp.dot(normed_attn, w_keyval, preferred_element_type=jnp.float32).astype(
        jnp.bfloat16
    )
    keyval_rows = jnp.transpose(ag_group(keyval_part, 2), (1, 0, 2)).reshape(local_rows, -1)
    query_proj = jnp.dot(normed_attn, w_query, preferred_element_type=jnp.float32)
    query_rot = rotary(query_proj.reshape(local_rows, heads_dev, HD), positions_local).astype(
        jnp.bfloat16
    )
    first_kv = group_index * heads_dev // group_size
    key_cols = lax.dynamic_slice_in_dim(keyval_rows, first_kv * HD, kv_dev * HD, 1)
    value_cols = lax.dynamic_slice_in_dim(keyval_rows, KVH * HD + first_kv * HD, kv_dev * HD, 1)
    needed = jnp.concatenate([key_cols, value_cols], axis=1)
    kv_all = ag_dp(needed, 3).reshape(-1, needed.shape[1])
    total_rows = kv_all.shape[0]
    key_pos = jnp.arange(total_rows, dtype=jnp.int32)
    key_rot = rotary(
        kv_all[:, : kv_dev * HD].astype(jnp.float32).reshape(total_rows, kv_dev, HD), key_pos
    ).astype(jnp.bfloat16)
    value_all = kv_all[:, kv_dev * HD :].reshape(total_rows, kv_dev, HD)
    query_grp = query_rot.reshape(local_rows, kv_dev, heads_dev // kv_dev, HD)
    scores = jnp.einsum(
        "rkgd,skd->kgrs", query_grp, key_rot, preferred_element_type=jnp.float32
    ) * HD ** (-0.5)
    allowed = key_pos[None, :] <= positions_local[:, None]
    scores = jnp.where(allowed[None, None, :, :], scores, -1e30)
    row_peak = jnp.max(scores, axis=-1, keepdims=True)
    expo_rows = jnp.exp(scores - row_peak)
    prob_rows = (expo_rows / jnp.sum(expo_rows, axis=-1, keepdims=True)).astype(jnp.bfloat16)
    attended = jnp.einsum(
        "kgrs,skd->rkgd", prob_rows, value_all, preferred_element_type=jnp.float32
    )
    attended = attended.astype(jnp.bfloat16).reshape(local_rows, heads_dev * HD)
    cols = w_gate.shape[0]
    gain = lax.dynamic_slice_in_dim(gain_mlp, data_index * cols, cols, 0)[None, :]
    return back(attended, full_rows, gain, w_out, w_gate, w_up, w_down, 4)


def solution(mesh):
    placed = (
        P("dp", ("section", "tensor")),
        P(),
        P(None, ("section", "tensor")),
        P(None, ("section", "tensor")),
        P(("section", "tensor"), None),
        P(),
        P("dp", ("section", "tensor")),
        P("dp", ("section", "tensor")),
        P(("section", "tensor"), "dp"),
    )
    return jax.shard_map(
        shards,
        mesh=mesh,
        in_specs=placed,
        out_specs=P(("section", "tensor"), "dp"),
        check_vma=False,
    )
```

time: 472 us -> 267 us (0.57)
  waiting for transfers between devices: 333 us -> 0 us
  Pallas kernels: 0 us -> 213 us
  blocking collectives: 61 us -> 0 us
  local copies, waits for them, and re-layouts: 3.47 us -> 33.3 us
  matrix products: 37.7 us -> 11.1 us
  between operations: 13.5 us -> 0.23 us
  other arithmetic: 17.5 us -> 7.72 us
    pallas_call x0 -> x4, Pallas kernels: none -> 213 us  [the longest x1 162 us: back(): pl.pallas_call(back_body, out_shape=jax.ShapeDtypeStruct((block, cols), B...]
    reduce_scatter x2 -> x0, waiting for transfers between devices: 146 us -> none  [the longest x1 87.3 us: shards(): lax.psum_scatter(jnp.concatenate([gate_block, up_block], axis=1), 'dp', s...]
    psum x1 -> x0, waiting for transfers between devices: 96.7 us -> none  [shards(): summed = lax.psum(head_terms, ('section', 'tensor'))]
    all_gather x2 -> x0, waiting for transfers between devices: 64.8 us -> none  [the longest x1 35.3 us: shards(): hidden_all = lax.all_gather(hidden_part, 'dp', axis=0, tiled=True)]
    all_gather x2 -> x0, blocking collectives: 33.5 us -> none  [the longest x1 26.3 us: shards(): lax.all_gather(keyval_part, ('section', 'tensor'), axis=1, tiled=True)]
    all_to_all x1 -> x0, blocking collectives: 27.5 us -> none  [shards(): lax.all_to_all(normed_mlp, 'dp', split_axis=1, concat_axis=0, tiled=True)]
    dot_general x4 -> x0, matrix products: 24.5 us -> none  [the longest x1 10.5 us: shards(): jnp.dot(row_block, w_down, preferred_element_type=jnp.float32)]
    all_to_all x1 -> x0, waiting for transfers between devices: 24.4 us -> none  [shards(): lax.all_to_all(mid_full, 'dp', split_axis=1, concat_axis=0, tiled=True)]
  transfers between devices with their start and end apart: 6 -> 0, of which waited for: 6 -> 0; matrix products, arithmetic and copies ran while one was open for 1% -> 0% of each run, Pallas kernels for 0% -> 0%
where the time goes in v1:
time: 267 us; the launch traced here: 266 us
  Pallas kernels  213 us (80%)
  local copies, waits for them, and re-layouts  33.3 us (12%)
  matrix products  11.1 us (4%)
  other arithmetic  7.72 us (3%)
    pallas_call x1, Pallas kernels, back(): pl.pallas_call(back_body, out_shape=jax.ShapeDtypeStruct((block, cols), B...  162 us
    pallas_call x2, Pallas kernels, ag_group(): pl.pallas_call(ag_group_body, out_shape=jax.ShapeDtypeStruct((size_s * si...  42.6 us
    dot_general x1, local copies, waits for them, and re-layouts, shards(): jnp.dot(normed_attn, w_query, preferred_element_type=jnp.float32)  21.4 us
    dot_general x1, matrix products, shards(): jnp.dot(normed_attn, w_query, preferred_element_type=jnp.float32)  8.72 us
    pallas_call x1, Pallas kernels, ag_dp(): pl.pallas_call(ag_dp_body, out_shape=jax.ShapeDtypeStruct((size_d,) + x.s...  8.09 us

profile of v1, /device:TPU:25, one launch (start us, length us, event | category | flops | bytes accessed | tf_op | source)
XLA Modules:
  0.0 265.6 jit_solution(273153582527959746)
XLA Ops:
  0.0 30.3 %shard_map.91 = bf16[8,128,1024]{2,1,0:T(8,128)(2,1)} custom-call(bf16[128,1024]{1,0:T(8,128)(2,1)} %x_ref.1), custom_call_target="tpu_custom_call" | custom-call | tf_op jit(solution)/shard_map/pallas_call | solution.py:121
  30.4 2.2 fusion
  32.6 2.0 fusion.2
  34.7 3.9 %copy.19 = bf16[128,8,1024]{0,2,1:T(8,128)(2,1)} copy(bf16[128,8,1024]{2,0,1:T(8,128)(2,1)} %fusion.2) | data formatting | bytes 4194304 | tf_op jit(solution)/shard_map/convert_element_type | solution.py:26
  38.6 21.4 %copy.32 = bf16[1024,8192]{1,0:T(8,128)(2,1)} copy(bf16[1024,8192]{0,1:T(8,128)(2,1)} %bitcast.48) | data formatting | bytes 33554432 | tf_op jit(solution)/shard_map/dot_general | solution.py:490
  60.0 8.7 %fusion.28 = f32[128,8,128]{0,2,1:T(8,128)S(1)} fusion(bf16[128,8192,1]{0,1,2:T(8,128)(2,1)} %bitcast.51, bf16[8,128,8192]{2,1,0:T(8,128)(2,1)} %bitcast.46), kind=kOutput, calls=%fused_computation.52 | convolution fusion | flops 2147483648 | bytes 19398656 | tf_op jit(solution)/shard_map/dot_general | solution.py:490
  68.8 0.2 multiply_cosine_fusion.1
  69.3 1.3 copy-done.1
  70.6 1.4 copy-done.4
  72.0 1.4 fusion.7.x_ref
  73.4 12.3 %shard_map.92 = bf16[8,128,256]{2,1,0:T(8,128)(2,1)} custom-call(bf16[128,256]{1,0:T(8,128)(2,1)} %fusion.7.x_ref), custom_call_target="tpu_custom_call" | custom-call | tf_op jit(solution)/shard_map/pallas_call | solution.py:121
  85.7 1.1 copy.35
  86.8 0.6 pad_maximum_fusion.x_ref
  87.5 8.1 %shard_map.93 = bf16[4,128,256]{2,1,0:T(8,128)(2,1)} custom-call(bf16[128,256]{1,0:T(8,128)(2,1)} %pad_maximum_fusion.x_ref), custom_call_target="tpu_custom_call" | custom-call | tf_op jit(solution)/shard_map/pallas_call | solution.py:150
  95.6 0.9 fusion.20
  96.5 1.2 fusion.24
  97.8 0.5 fusion.27
  98.3 0.3 fusion.6
  98.7 0.5 convolution_convert_fusion
  99.3 0.9 copy.33.att_ref
  100.1 0.7 dynamic_slice.11
  100.8 0.6 broadcast_in_dim.12.gain_ref
  101.4 162.5 %shard_map.94 = bf16[64,2048]{1,0:T(8,128)(2,1)} custom-call(bf16[128,1024]{1,0:T(8,128)(2,1)} %copy.33.att_ref, bf16[128,8192]{1,0:T(8,128)(2,1)} %bitcast.50, bf16[1,2048]{1,0:T(2,128)(2,1)} %broadcast_in_dim.12.gain_ref, bf16[1024,8192]{1,0:T(8,128)(2,1)} %wo_hbm.1, bf16[2048,2048]{1,0:T(8,128)(2,1)} %wg_hbm.1, bf16[2048,2048]{1,0:T(8,128)(2,1)} %wu_hbm.1, ...), custom_call_target="tpu_custom_call" | custom-call | tf_op jit(solution)/shard_map/pallas_call | solution.py:430
  263.9 1.7 copy.37
  (18 shorter events, 0.5 us)
Async XLA Ops:
  0.0 30.3 %copy-start.3 = (bf16[8192]{0:T(1024)(128)(2,1)S(1)}, bf16[8192]{0:T(1024)(128)(2,1)}, u32[]{:S(2)}) copy-start(bf16[8192]{0:T(1024)(128)(2,1)} %param.10) | copy-start | bytes 49156
  30.4 2.3 copy-start
  69.0 2.9 %copy-start.4 = (bf16[8192,256]{1,0:T(8,128)(2,1)S(1)}, bf16[8192,256]{1,0:T(8,128)(2,1)}, u32[]{:S(2)}) copy-start(bf16[8192,256]{1,0:T(8,128)(2,1)} %param.12) | copy-start | bytes 12582916
  69.2 1.3 copy-start.1
  97.8 1.0 copy-start.2

commit v2 on v1

--- a/solution.py
+++ b/solution.py
@@ -1,5 +1,3 @@
-import functools
-
 import jax
 import jax.numpy as jnp
 from jax import lax
@@ -20,26 +18,6 @@
 ANY = pl.BlockSpec(memory_space=pl.ANY)
 
 
-def rms_scale(row_data, gain_row):
-    values = row_data.astype(jnp.float32)
-    factor = lax.rsqrt(jnp.mean(values * values, axis=-1, keepdims=True) + EPS)
-    return (values * factor * gain_row.astype(jnp.float32)).astype(jnp.bfloat16)
-
-
-def rotary(values, positions):
-    half_dim = values.shape[-1] // 2
-    frequency = THETA ** (-jnp.arange(half_dim, dtype=jnp.float32) * 2.0 / values.shape[-1])
-    angles = positions.astype(jnp.float32)[:, None] * frequency[None, :]
-    cosine = jnp.cos(angles)[:, None, :]
-    sine_part = jnp.sin(angles)[:, None, :]
-    first_half = values[..., :half_dim]
-    second = values[..., half_dim:]
-    return jnp.concatenate(
-        [first_half * cosine - second * sine_part, second * cosine + first_half * sine_part],
-        axis=-1,
-    )
-
-
 def greet(peers):
     barrier = pltpu.get_barrier_semaphore()
     for peer in peers:
@@ -64,7 +42,7 @@
     return [(step, lax.rem(me + step, size), lax.rem(me + size - step, size)) for step in range(1, size)]
 
 
-def gather_group(out, at, sem_t, sem_s):
+def gather_group(out, at, sem_t, sem_s, on_block=lambda section, tensor, order: None):
     section, tensor = lax.axis_index("section"), lax.axis_index("tensor")
     sections, tensors = others("section"), others("tensor")
     size_t = lax.axis_size("tensor")
@@ -83,15 +61,25 @@
         copy.start()
         started.append(copy)
     pass_on(tensor, 0)
-    for step, to, source in tensors:
-        block = out.at[at(section, source)]
-        push(block, block, sem_t, step - 1, {"tensor": to}).wait_recv()
-        pass_on(source, step)
-    for slot in range(size_t):
+    on_block(section, tensor, 0)
+
+    def from_sections(slot):
         for step, to, source in sections:
             source_t = lax.rem(tensor + size_t - slot, size_t)
             block = out.at[at(source, source_t)]
             push(block, block, sem_s, slot * len(sections) + step - 1, {"section": to}).wait_recv()
+            on_block(source, source_t, (slot + 1) * len(sections) + slot + step - 1)
+
+    for step, to, source in tensors:
+        if step == 1:
+            from_sections(0)
+        block = out.at[at(section, source)]
+        push(block, block, sem_t, step - 1, {"tensor": to}).wait_recv()
+        pass_on(source, step)
+        on_block(section, source, step * (len(sections) + 1))
+        if step > 1:
+            from_sections(step - 1)
+    from_sections(size_t - 1)
     for copy in started:
         copy.wait_send()
 
@@ -106,55 +94,232 @@
     return pltpu.SemaphoreType.DMA((2, max(1, count)))
 
 
-def ag_group_body(x_ref, out_ref, sem_t, sem_s, sem_local):
+def block_order():
     section, tensor = lax.axis_index("section"), lax.axis_index("tensor")
     size_t = lax.axis_size("tensor")
-    greet(group_peers())
-    own = pltpu.make_async_copy(x_ref, out_ref.at[section * size_t + tensor], sem_local)
+
+    def from_sections(slot):
+        return [(source, lax.rem(tensor + size_t - slot, size_t)) for _, _, source in others("section")]
+
+    order = [(section, tensor)] + from_sections(0)
+    for step, _, source in others("tensor"):
+        order.append((section, source))
+        if step > 1:
+            order += from_sections(step - 1)
+    return order + from_sections(size_t - 1)
+
+
+def front_body(
+    x_ref, gain_ref, cos_ref, sin_ref, wq_hbm, wk_hbm, att_ref, full_ref,
+    blocks, wq, wk, qacc, kacc, stat, kv_src, kv_dst,
+    sem_w, sem_own, sem_t, sem_s, sem_kv, sem_kv_out,
+):
+    section, tensor, me = lax.axis_index("section"), lax.axis_index("tensor"), lax.axis_index("dp")
+    size_s, size_t, size_d = lax.axis_size("section"), lax.axis_size("tensor"), lax.axis_size("dp")
+    count = size_s * size_t
+    index = section * size_t + tensor
+    local_rows, width = x_ref.shape
+    features = count * width
+    heads_dev = qacc.shape[1] // HD
+    group_size = H // KVH
+    units, _, unit = kv_src.shape
+    pieces = HD // unit
+    rep = group_size // heads_dev
+
+    order = block_order()
+    loads = []
+    for k, (s, t) in enumerate(order):
+        rows = pl.ds(pl.multiple_of((s * size_t + t) * width, width), width)
+        loads.append(
+            (
+                pltpu.make_async_copy(wq_hbm.at[rows], wq.at[k], sem_w.at[0, k]),
+                pltpu.make_async_copy(wk_hbm.at[rows], wk.at[k], sem_w.at[1, k]),
+            )
+        )
+    for pair in loads:
+        for load in pair:
+            load.start()
+    own = pltpu.make_async_copy(x_ref, blocks.at[index], sem_own)
     own.start()
+
+    dps = others("dp")
+    everyone = []
+    for hop_s in range(size_s):
+        for hop_t in range(size_t):
+            for hop_d in range(size_d):
+                if hop_s + hop_t + hop_d:
+                    everyone.append(
+                        {
+                            "section": lax.rem(section + hop_s, size_s),
+                            "tensor": lax.rem(tensor + hop_t, size_t),
+                            "dp": lax.rem(me + hop_d, size_d),
+                        }
+                    )
+    greet(everyone)
     own.wait()
-    gather_group(out_ref, lambda s, t: s * size_t + t, sem_t, sem_s)
-
-
-def ag_group(x, collective_id):
-    size_s, size_t = lax.axis_size("section"), lax.axis_size("tensor")
+
+    seen = []
+
+    def on_block(s, t, _):
+        k = len(seen)
+        seen.append(k)
+        for load in loads[k]:
+            load.wait()
+        at = s * size_t + t
+        raw = blocks[at]
+        full_ref[:, pl.ds(pl.multiple_of(at * width, width), width)] = raw
+        rows = raw.astype(F32)
+        part = jnp.sum(rows * rows, axis=-1, keepdims=True)
+        stat[...] = part if k == 0 else stat[...] + part
+        scaled = (rows * gain_ref[at].astype(F32)).astype(BF16)
+        tile = tile_of(qacc.shape[1], 256)
+
+        @pl.loop(0, qacc.shape[1] // tile)
+        def _(j):
+            cols = pl.ds(pl.multiple_of(j * tile, tile), tile)
+            term = jnp.dot(scaled, wq[k, :, cols], preferred_element_type=F32)
+            qacc[:, cols] = term if k == 0 else qacc[:, cols] + term
+
+        term = jnp.dot(scaled, wk[k], preferred_element_type=F32)
+        kacc[...] = term if k == 0 else kacc[...] + term
+
+    gather_group(blocks, lambda s, t: s * size_t + t, sem_t, sem_s, on_block)
+    factor = lax.rsqrt(stat[...] * (1.0 / features) + EPS)
+
+    for i in range(units):
+        kv_src[i] = (kacc[:, i * unit : (i + 1) * unit] * factor).astype(BF16)
+
+    def dp_rows(at):
+        return pl.ds(pl.multiple_of(at * local_rows, local_rows), local_rows)
+
+    half = KVH * pieces
+
+    def kv_copy(i, r, g, kind, piece, step, to):
+        return pltpu.make_async_remote_copy(
+            src_ref=kv_src.at[i],
+            dst_ref=kv_dst.at[kind, piece, dp_rows(me)],
+            send_sem=sem_kv_out.at[(i * rep + r) * size_d + step],
+            recv_sem=sem_kv.at[1, (kind * pieces + piece) * size_d + step],
+            device_id={"section": g // size_t, "tensor": lax.rem(g, size_t), "dp": to},
+            device_id_type=MESH,
+        )
+
+    hops = [(step, to, source) for step, to, source in dps] + [(0, me, me)]
+
+    def each_send(act):
+        for i in range(units):
+            u = index * units + i
+            kind, piece = u // half, lax.rem(u, pieces)
+            head = lax.rem(u, half) // pieces
+            for r in range(rep):
+                g = head * rep + r
+                for step, to, _ in hops:
+                    if step:
+                        act(kv_copy(i, r, g, kind, piece, step, to), i, kind, piece, False)
+                    else:
+                        @pl.when(g != index)
+                        def _():
+                            act(kv_copy(i, r, g, kind, piece, step, to), i, kind, piece, False)
+
+                        @pl.when(g == index)
+                        def _():
+                            act(None, i, kind, piece, True)
+
+    def begin(copy, i, kind, piece, local):
+        if local:
+            kv_dst[kind, piece, dp_rows(me), :] = kv_src[i]
+        else:
+            copy.start()
+
+    each_send(begin)
+
+    cosine, sine = cos_ref[dp_rows(me), :], sin_ref[dp_rows(me), :]
+    queries = []
+    for h in range(heads_dev):
+        q = qacc[:, h * HD : (h + 1) * HD] * factor
+        q = q * cosine + pltpu.roll(q, HD // 2, axis=1) * sine
+        queries.append(q.astype(BF16))
+
+    head = index // rep
+    for kind in range(2):
+        for piece in range(pieces):
+            g = (kind * half + head * pieces + piece) // units
+            for step, to, source in hops:
+                dst = kv_dst.at[kind, piece, dp_rows(source)]
+                wait = push(dst, dst, sem_kv, (kind * pieces + piece) * size_d + step, {"tensor": tensor})
+                if step:
+                    wait.wait_recv()
+                else:
+                    @pl.when(g != index)
+                    def _():
+                        wait.wait_recv()
+
+    def whole(kind):
+        return jnp.concatenate([kv_dst[kind, piece] for piece in range(pieces)], axis=1) if pieces > 1 else kv_dst[kind, 0]
+
+    keys = whole(0).astype(F32)
+    keys = (keys * cos_ref[...] + pltpu.roll(keys, HD // 2, axis=1) * sin_ref[...]).astype(BF16)
+    values = whole(1)
+    total_rows = keys.shape[0]
+    shape = (local_rows, total_rows)
+    allowed = lax.broadcasted_iota(jnp.int32, shape, 1) <= (
+        lax.broadcasted_iota(jnp.int32, shape, 0) + me * local_rows
+    )
+    for h in range(heads_dev):
+        scores = lax.dot_general(
+            queries[h], keys, (((1,), (1,)), ((), ())), preferred_element_type=F32
+        ) * HD ** (-0.5)
+        scores = jnp.where(allowed, scores, -1e30)
+        expo = jnp.exp(scores - jnp.max(scores, axis=-1, keepdims=True))
+        probs = (expo / jnp.sum(expo, axis=-1, keepdims=True)).astype(BF16)
+        att_ref[:, h * HD : (h + 1) * HD] = jnp.dot(
+            probs, values, preferred_element_type=F32
+        ).astype(BF16)
+
+    def end(copy, i, kind, piece, local):
+        if not local:
+            copy.wait_send()
+
+    each_send(end)
+
+
+def front(tokens, gain, cosine, sine, w_query, w_keyval, collective_id):
+    size_s, size_t, size_d = lax.axis_size("section"), lax.axis_size("tensor"), lax.axis_size("dp")
+    count = size_s * size_t
+    local_rows, width = tokens.shape
+    kv_cols = w_keyval.shape[1]
+    unit = min(kv_cols, HD)
+    pieces = HD // unit
+    rep = (H // KVH) // (w_query.shape[1] // HD)
+    arrivals = 2 * pieces * size_d
     return pl.pallas_call(
-        ag_group_body,
-        out_shape=jax.ShapeDtypeStruct((size_s * size_t,) + x.shape, x.dtype),
-        in_specs=[VMEM],
-        out_specs=VMEM,
-        scratch_shapes=[dma_sems(size_t - 1), dma_sems(size_t * (size_s - 1)), pltpu.SemaphoreType.DMA],
-        compiler_params=pltpu.CompilerParams(collective_id=collective_id, has_side_effects=True),
-    )(x)
-
-
-def ag_dp_body(x_ref, out_ref, sem_d, sem_local):
-    me = lax.axis_index("dp")
-    greet([{"dp": to} for _, to, _ in others("dp")])
-    own = pltpu.make_async_copy(x_ref, out_ref.at[me], sem_local)
-    own.start()
-    copies = []
-    for step, to, _ in others("dp"):
-        copy = push(x_ref, out_ref.at[me], sem_d, step - 1, {"dp": to})
-        copy.start()
-        copies.append(copy)
-    own.wait()
-    for step, to, source in others("dp"):
-        push(x_ref, out_ref.at[source], sem_d, step - 1, {"dp": to}).wait_recv()
-    for copy in copies:
-        copy.wait_send()
-
-
-def ag_dp(x, collective_id):
-    size_d = lax.axis_size("dp")
-    return pl.pallas_call(
-        ag_dp_body,
-        out_shape=jax.ShapeDtypeStruct((size_d,) + x.shape, x.dtype),
-        in_specs=[VMEM],
-        out_specs=VMEM,
-        scratch_shapes=[dma_sems(size_d - 1), pltpu.SemaphoreType.DMA],
-        compiler_params=pltpu.CompilerParams(collective_id=collective_id, has_side_effects=True),
-    )(x)
+        front_body,
+        out_shape=(
+            jax.ShapeDtypeStruct((local_rows, w_query.shape[1]), BF16),
+            jax.ShapeDtypeStruct((local_rows, count * width), BF16),
+        ),
+        in_specs=[VMEM, VMEM, VMEM, VMEM, ANY, ANY],
+        out_specs=(VMEM, VMEM),
+        scratch_shapes=[
+            pltpu.VMEM((count, local_rows, width), BF16),
+            pltpu.VMEM((count, width, w_query.shape[1]), BF16),
+            pltpu.VMEM((count, width, kv_cols), BF16),
+            pltpu.VMEM((local_rows, w_query.shape[1]), F32),
+            pltpu.VMEM((local_rows, kv_cols), F32),
+            pltpu.VMEM((local_rows, 1), F32),
+            pltpu.VMEM((kv_cols // unit, local_rows, unit), BF16),
+            pltpu.VMEM((2, pieces, local_rows * size_d, unit), BF16),
+            pltpu.SemaphoreType.DMA((2, count)),
+            pltpu.SemaphoreType.DMA,
+            dma_sems(size_t - 1),
+            dma_sems(size_t * (size_s - 1)),
+            dma_sems(arrivals),
+            pltpu.SemaphoreType.DMA((kv_cols // unit * rep * size_d,)),
+        ],
+        compiler_params=pltpu.CompilerParams(
+            collective_id=collective_id, has_side_effects=True, vmem_limit_bytes=66000000
+        ),
+    )(tokens, gain, cosine, sine, w_query, w_keyval)
 
 
 def tile_of(width, most):
@@ -473,51 +638,25 @@
 
 
 def shards(tokens_in, gain_attn, w_query, w_keyval, w_out, gain_mlp, w_gate, w_up, w_down):
-    group_index = lax.axis_index(("section", "tensor"))
     data_index = lax.axis_index("dp")
-    local_rows = tokens_in.shape[0]
-    gathered = ag_group(tokens_in, 1)
-    full_rows = jnp.transpose(gathered, (1, 0, 2)).reshape(local_rows, -1)
-    normed_attn = rms_scale(full_rows, gain_attn)
-    heads_dev = w_query.shape[1] // HD
-    group_size = H // KVH
-    kv_dev = max(1, heads_dev // group_size)
-    positions_local = data_index * local_rows + jnp.arange(local_rows, dtype=jnp.int32)
-    keyval_part = jnp.dot(normed_attn, w_keyval, preferred_element_type=jnp.float32).astype(
-        jnp.bfloat16
+    local_rows, width = tokens_in.shape
+    total_rows = local_rows * lax.axis_size("dp")
+    half_dim = HD // 2
+    frequency = THETA ** (-jnp.arange(half_dim, dtype=jnp.float32) * 2.0 / HD)
+    angles = jnp.arange(total_rows, dtype=jnp.int32).astype(F32)[:, None] * frequency[None, :]
+    cosine, sine = jnp.cos(angles), jnp.sin(angles)
+    attended, full_rows = front(
+        tokens_in,
+        gain_attn.reshape(-1, 1, width),
+        jnp.concatenate([cosine, cosine], axis=1),
+        jnp.concatenate([-sine, sine], axis=1),
+        w_query,
+        w_keyval,
+        1,
     )
-    keyval_rows = jnp.transpose(ag_group(keyval_part, 2), (1, 0, 2)).reshape(local_rows, -1)
-    query_proj = jnp.dot(normed_attn, w_query, preferred_element_type=jnp.float32)
-    query_rot = rotary(query_proj.reshape(local_rows, heads_dev, HD), positions_local).astype(
-        jnp.bfloat16
-    )
-    first_kv = group_index * heads_dev // group_size
-    key_cols = lax.dynamic_slice_in_dim(keyval_rows, first_kv * HD, kv_dev * HD, 1)
-    value_cols = lax.dynamic_slice_in_dim(keyval_rows, KVH * HD + first_kv * HD, kv_dev * HD, 1)
-    needed = jnp.concatenate([key_cols, value_cols], axis=1)
-    kv_all = ag_dp(needed, 3).reshape(-1, needed.shape[1])
-    total_rows = kv_all.shape[0]
-    key_pos = jnp.arange(total_rows, dtype=jnp.int32)
-    key_rot = rotary(
-        kv_all[:, : kv_dev * HD].astype(jnp.float32).reshape(total_rows, kv_dev, HD), key_pos
-    ).astype(jnp.bfloat16)
-    value_all = kv_all[:, kv_dev * HD :].reshape(total_rows, kv_dev, HD)
-    query_grp = query_rot.reshape(local_rows, kv_dev, heads_dev // kv_dev, HD)
-    scores = jnp.einsum(
-        "rkgd,skd->kgrs", query_grp, key_rot, preferred_element_type=jnp.float32
-    ) * HD ** (-0.5)
-    allowed = key_pos[None, :] <= positions_local[:, None]
-    scores = jnp.where(allowed[None, None, :, :], scores, -1e30)
-    row_peak = jnp.max(scores, axis=-1, keepdims=True)
-    expo_rows = jnp.exp(scores - row_peak)
-    prob_rows = (expo_rows / jnp.sum(expo_rows, axis=-1, keepdims=True)).astype(jnp.bfloat16)
-    attended = jnp.einsum(
-        "kgrs,skd->rkgd", prob_rows, value_all, preferred_element_type=jnp.float32
-    )
-    attended = attended.astype(jnp.bfloat16).reshape(local_rows, heads_dev * HD)
     cols = w_gate.shape[0]
     gain = lax.dynamic_slice_in_dim(gain_mlp, data_index * cols, cols, 0)[None, :]
-    return back(attended, full_rows, gain, w_out, w_gate, w_up, w_down, 4)
+    return back(attended, full_rows, gain, w_out, w_gate, w_up, w_down, 2)
 
 
 def solution(mesh):

time: 267 us -> 215 us (0.81)
  local copies, waits for them, and re-layouts: 33.3 us -> 4.3 us
  matrix products: 11.1 us -> 0 us
  other arithmetic: 7.72 us -> 2.01 us
  Pallas kernels: 213 us -> 209 us
    dot_general x1 -> x0, local copies, waits for them, and re-layouts: 21.4 us -> none  [shards(): jnp.dot(normed_attn, w_query, preferred_element_type=jnp.float32)]
    dot_general x4 -> x0, matrix products: 11.1 us -> none  [the longest x1 8.72 us: shards(): jnp.dot(normed_attn, w_query, preferred_element_type=jnp.float32)]
    pallas_call x3 -> x1, Pallas kernels: 50.7 us -> 45.7 us  [front(): pl.pallas_call(front_body, out_shape=(jax.ShapeDtypeStruct((local_rows, w...]
    convert_element_type x1 -> x0, local copies, waits for them, and re-layouts: 3.91 us -> none  [rms_scale(): return (values * factor * gain_row.astype(jnp.float32)).astype(jnp.bfloat16)]
    unnamed x11 -> x1, local copies, waits for them, and re-layouts: 4.56 us -> 1.67 us
where the time goes in v2:
time: 215 us
  Pallas kernels  209 us (97%)
  local copies, waits for them, and re-layouts  4.3 us (2%)
    pallas_call x1, Pallas kernels, back(): pl.pallas_call(back_body, out_shape=jax.ShapeDtypeStruct((block, cols), B...  163 us
    pallas_call x1, Pallas kernels, front(): pl.pallas_call(front_body, out_shape=(jax.ShapeDtypeStruct((local_rows, w...  45.7 us

profile of v2, /device:TPU:25, one launch (start us, length us, event | category | flops | bytes accessed | tf_op | source)
XLA Modules:
  0.0 215.0 jit_solution(5238716452527371618)
XLA Ops:
  0.0 1.0 fusion
  1.0 1.0 pad_maximum_fusion
  2.0 1.3 reshape.14.gain_ref
  3.4 45.7 %shard_map.91 = (bf16[128,1024]{1,0:T(8,128)(2,1)}, bf16[128,8192]{1,0:T(8,128)(2,1)}) custom-call(bf16[128,1024]{1,0:T(8,128)(2,1)} %x_ref.1, bf16[8,1,1024]{2,1,0:T(2,128)(2,1)} %reshape.14.gain_ref, f32[512,128]{1,0:T(8,128)} %get-tuple-element.12.cos_ref, f32[512,128]{1,0:T(8,128)} %get-tuple-element.13.sin_ref, bf16[8192,1024]{1,0:T(8,128)(2,1)} %wq_hbm.1, ...), custom_call_target="tpu_custom_call" | custom-call | tf_op jit(solution)/shard_map/pallas_call | solution.py:295
  49.1 0.7 dynamic_slice.3
  49.8 0.6 broadcast_in_dim.2.gain_ref
  50.4 163.0 %shard_map.92 = bf16[64,2048]{1,0:T(8,128)(2,1)} custom-call(bf16[128,1024]{1,0:T(8,128)(2,1)} %get-tuple-element.7.att_ref, bf16[128,8192]{1,0:T(8,128)(2,1)} %get-tuple-element.8.rows_ref, bf16[1,2048]{1,0:T(2,128)(2,1)} %broadcast_in_dim.2.gain_ref, bf16[1024,8192]{1,0:T(8,128)(2,1)} %wo_hbm.1, bf16[2048,2048]{1,0:T(8,128)(2,1)} %wg_hbm.1, ...), custom_call_target="tpu_custom_call" | custom-call | tf_op jit(solution)/shard_map/pallas_call | solution.py:595
  213.3 1.7 copy.12
  (2 shorter events, 0.0 us)

commit v3 on v2

--- a/solution.py
+++ b/solution.py
@@ -10,7 +10,7 @@
 HD = 128
 EPS = 1e-05
 THETA = 10000.0
-CHUNKS = 4
+CHUNKS = 8
 MESH = pl.DeviceIdType.MESH
 F32 = jnp.float32
 BF16 = jnp.bfloat16
@@ -390,6 +390,7 @@
     block, cols = mid.shape
     total_rows = att_all.shape[0]
     features = rows_ref.shape[1]
+    chunks = gu.shape[0]
     dps = others("dp")
     sends = []
 
@@ -486,7 +487,7 @@
         x, y = lax.rem(me, 2), me // 2
         near = [y * 2 + (1 - x), (1 - y) * 2 + x]
         far = (1 - y) * 2 + (1 - x)
-    for c in range(CHUNKS):
+    for c in range(chunks):
         @pl.loop(0, share // gtile)
         def _(j):
             src = pl.ds(pl.multiple_of(c * share + j * gtile, gtile), gtile)
@@ -509,7 +510,7 @@
                 sends.append(copy)
 
     if square:
-        for c in range(CHUNKS):
+        for c in range(chunks):
             first, second = near[c % 2], near[1 - c % 2]
             push(gu.at[c, dp_rows(far)], rx1.at[c, 1], sem_1, 2 * c + 1, {"dp": first}).wait_recv()
             tx2[c] = (gu[c, dp_rows(second), :].astype(F32) + rx1[c, 1].astype(F32)).astype(BF16)
@@ -518,7 +519,7 @@
             sends.append(copy)
 
     hid_slots = size_d - 1
-    for c in range(CHUNKS):
+    for c in range(chunks):
         both = gu[c, dp_rows(me), :].astype(F32)
         if square:
             first, second = near[c % 2], near[1 - c % 2]
@@ -542,7 +543,7 @@
             sends.append(copy)
 
     if square:
-        for c in range(CHUNKS):
+        for c in range(chunks):
             one, two = c % 2, 1 - c % 2
             theirs = hid.at[c, dp_rows(near[one])]
             push(theirs, theirs, sem_h, hid_slots * c + one, {"dp": near[one]}).wait_recv()
@@ -551,7 +552,7 @@
             sends.append(copy)
 
     loads[3].wait()
-    for c in range(CHUNKS):
+    for c in range(chunks):
         if square:
             two = 1 - c % 2
             arrivals = [(two, near[two]), (2, far)]
@@ -567,7 +568,7 @@
             term = jnp.dot(hid[c], wd[c * share : (c + 1) * share, at], preferred_element_type=F32)
             if c > 0:
                 term = acc[:, at] + term
-            if c < CHUNKS - 1:
+            if c < chunks - 1:
                 acc[:, at] = term
             else:
                 part2[:, at] = term.astype(BF16)
@@ -584,7 +585,8 @@
     total_rows = local_rows * size_d
     block = total_rows // (size_s * size_t)
     cols, hidden = w_gate.shape
-    share = hidden // CHUNKS
+    chunks = min(CHUNKS, hidden // 128)
+    share = hidden // chunks
     slots = 2 if size_d == 4 else size_d - 1
     scatter = [
         pltpu.VMEM((total_rows, cols), BF16),
@@ -609,11 +611,11 @@
             pltpu.VMEM((block, 128), F32),
             pltpu.VMEM((size_d - 1, block, 128), F32),
             pltpu.VMEM((total_rows, cols), BF16),
-            pltpu.VMEM((CHUNKS, total_rows, 2 * share), BF16),
-            pltpu.VMEM((CHUNKS, slots, local_rows, 2 * share), BF16),
-            pltpu.VMEM((CHUNKS, local_rows, 2 * share), BF16),
-            pltpu.VMEM((CHUNKS, local_rows, 2 * share), BF16),
-            pltpu.VMEM((CHUNKS, total_rows, share), BF16),
+            pltpu.VMEM((chunks, total_rows, 2 * share), BF16),
+            pltpu.VMEM((chunks, slots, local_rows, 2 * share), BF16),
+            pltpu.VMEM((chunks, local_rows, 2 * share), BF16),
+            pltpu.VMEM((chunks, local_rows, 2 * share), BF16),
+            pltpu.VMEM((chunks, total_rows, share), BF16),
             pltpu.VMEM((total_rows, cols), F32),
             *scatter,
             pltpu.SemaphoreType.DMA((4,)),
@@ -625,9 +627,9 @@
             dma_sems(size_d - 1),
             dma_sems(size_t - 1),
             dma_sems(size_t * (size_s - 1)),
-            dma_sems(CHUNKS * slots),
-            dma_sems(CHUNKS),
-            dma_sems(CHUNKS * (size_d - 1)),
+            dma_sems(chunks * slots),
+            dma_sems(chunks),
+            dma_sems(chunks * (size_d - 1)),
             dma_sems((size_s - 1) * size_t),
             dma_sems(size_t - 1),
         ],

time: 215 us -> 214 us (level)
  no operation moved by 1% of the time
where the time goes in v3:
time: 214 us
  Pallas kernels  208 us (97%)
  local copies, waits for them, and re-layouts  4.3 us (2%)
    pallas_call x1, Pallas kernels, back(): pl.pallas_call(back_body, out_shape=jax.ShapeDtypeStruct((block, cols), B...  162 us
    pallas_call x1, Pallas kernels, front(): pl.pallas_call(front_body, out_shape=(jax.ShapeDtypeStruct((local_rows, w...  45.7 us

profile of v3, /device:TPU:25, one launch (start us, length us, event | category | flops | bytes accessed | tf_op | source)
XLA Modules:
  0.0 213.9 jit_solution(15017062883783523787)
XLA Ops:
  0.0 1.0 fusion
  1.0 1.0 pad_maximum_fusion
  2.0 1.3 reshape.14.gain_ref
  3.4 45.7 %shard_map.91 = (bf16[128,1024]{1,0:T(8,128)(2,1)}, bf16[128,8192]{1,0:T(8,128)(2,1)}) custom-call(bf16[128,1024]{1,0:T(8,128)(2,1)} %x_ref.1, bf16[8,1,1024]{2,1,0:T(2,128)(2,1)} %reshape.14.gain_ref, f32[512,128]{1,0:T(8,128)} %get-tuple-element.12.cos_ref, f32[512,128]{1,0:T(8,128)} %get-tuple-element.13.sin_ref, bf16[8192,1024]{1,0:T(8,128)(2,1)} %wq_hbm.1, ...), custom_call_target="tpu_custom_call" | custom-call | tf_op jit(solution)/shard_map/pallas_call | solution.py:295
  49.1 0.7 dynamic_slice.3
  49.8 0.6 broadcast_in_dim.2.gain_ref
  50.4 161.8 %shard_map.92 = bf16[64,2048]{1,0:T(8,128)(2,1)} custom-call(bf16[128,1024]{1,0:T(8,128)(2,1)} %get-tuple-element.7.att_ref, bf16[128,8192]{1,0:T(8,128)(2,1)} %get-tuple-element.8.rows_ref, bf16[1,2048]{1,0:T(2,128)(2,1)} %broadcast_in_dim.2.gain_ref, bf16[1024,8192]{1,0:T(8,128)(2,1)} %wo_hbm.1, bf16[2048,2048]{1,0:T(8,128)(2,1)} %wg_hbm.1, ...), custom_call_target="tpu_custom_call" | custom-call | tf_op jit(solution)/shard_map/pallas_call | solution.py:597
  212.2 1.7 copy.12
  (2 shorter events, 0.0 us)
